TPU v7x, 32 devices: a whole 2x2x4 slice. The times are simulated.
32 devices in a mesh: grp: 8 (over z, x), node: 4 (over y, core).
Axes of the slice: x: 2, y: 2, z: 4, core: 2. Of those that a mesh axis runs over, the one named last changes fastest.
Arguments:
- initial: float32 [6, 32, 32768], P(None, None, ('grp', 'node')), may hold values from -0.5 to 16, as said below
- afferent_noise_level: float32 [32, 32768], P(None, ('grp', 'node')), may hold values from 0.12 to 0.32
- history: bfloat16 [64, 32, 32768], P(None, None, ('grp', 'node')), may hold values from 0 to 1
- weights: bfloat16 [32, 24, 128, 1024], P(('grp', 'node')), may hold values from -0.109375 to 0.109375
- lead_field: bfloat16 [128, 32768], P(None, ('grp', 'node')), may hold values from -0.00390625 to 0.00390625
- src_group: int32 [32, 24], replicated, may hold values from 0 to 7, as said below
- src_sub: int32 [32, 24], replicated, may hold values from 0 to 7
- delays: int32 [32, 24], replicated, may hold values from 6 to 63
- counts: int32 [32], replicated, may hold values from 16 to 24, as said below
Outputs:
- final_state: float32 [6, 32, 32768], P(None, None, ('grp', 'node'))
- sensors: float32 [6, 128, 32], replicated
Inputs may be any that keep to these rules, and one draw needn't show every extreme that they name: `initial`: rows 0 to 2 are potentials and rows 3 to 5 their rates; row 0 lies within 0 and 0.4, row 1 within 4 and 16, row 2 within 0 and 8, rows 3 to 5 within -0.5 and 0.5. `src_group`: among the tiles k < counts[b] of a block b no owner group appears more than 3 times, and some block reaches 3. Tiles k >= counts[b] of block b are ignored; in every draw some block has 24 live tiles.
All inputs are finite; a program needn't handle non-finite values.
Results may differ from a plain program's by a relative error of at most 0.0003.
The roundings to bfloat16 on the way count: a program that leaves them out, or rounds other values in their place, can miss the bound.
Values may be sent and summed in bfloat16 or wider, within the bound.
A program may use at most 128 MiB of HBM per device.

v0:
```python
import jax
import jax.numpy as jnp
from jax import lax
from jax.sharding import PartitionSpec as P

DMIN = 6
STEPS = 6


exciting_amplitude = 3.25
suppressive_amplitude = 22.0
exciting_inverse_lag = 0.1
suppressive_inverse_lag = 0.05
link_factor = 135.0
maximal_spike_frequency = 0.005
thresh = 6.0
fire_slope = 0.56
global_scaling_factor = 0.5
dt_step = 0.5


def sigmoid_spike_density(somatic_charge_level):
    return 1.0 / (1.0 + jnp.exp(fire_slope * (thresh - somatic_charge_level)))


def derivative(population_variables, afferent_noise_level, network_afferent):
    principal_cell_level, interneuron_depolarization, suppressive_depolarization = (
        population_variables[0],
        population_variables[1],
        population_variables[2],
    )
    principal_cell_curvature = (
        exciting_amplitude
        * exciting_inverse_lag
        * maximal_spike_frequency
        * sigmoid_spike_density(interneuron_depolarization - suppressive_depolarization)
        - 2.0 * exciting_inverse_lag * population_variables[3]
        - exciting_inverse_lag * exciting_inverse_lag * principal_cell_level
    )
    interneuron_second_derivative = (
        exciting_amplitude
        * exciting_inverse_lag
        * (
            afferent_noise_level
            + 0.8
            * link_factor
            * maximal_spike_frequency
            * sigmoid_spike_density(link_factor * principal_cell_level)
            + global_scaling_factor * network_afferent
        )
        - 2.0 * exciting_inverse_lag * population_variables[4]
        - exciting_inverse_lag * exciting_inverse_lag * interneuron_depolarization
    )
    suppressive_second_derivative = (
        suppressive_amplitude
        * suppressive_inverse_lag
        * 0.25
        * link_factor
        * maximal_spike_frequency
        * sigmoid_spike_density(0.25 * link_factor * principal_cell_level)
        - 2.0 * suppressive_inverse_lag * population_variables[5]
        - suppressive_inverse_lag * suppressive_inverse_lag * suppressive_depolarization
    )
    return jnp.stack(
        [
            population_variables[3],
            population_variables[4],
            population_variables[5],
            principal_cell_curvature,
            interneuron_second_derivative,
            suppressive_second_derivative,
        ]
    )


def advance(population_variables, afferent_noise_level, coupled_now, coupled_next):
    first_rate = derivative(population_variables, afferent_noise_level, coupled_now)
    second_rate = derivative(
        population_variables + dt_step * first_rate, afferent_noise_level, coupled_next
    )
    return population_variables + 0.5 * dt_step * (first_rate + second_rate)


def body(
    initial, afferent_noise_level, history, weights, lead_field, src_group, src_sub, delays, counts
):
    owners = lax.axis_size("grp")
    columns = lax.axis_size("node")
    my_group = lax.axis_index("grp")
    my_column = lax.axis_index("node")
    myself = my_group * columns + my_column
    cycle_len, replicas, block_len = history.shape
    tiles_max = src_group.shape[1]
    piece_len = weights.shape[2]
    slots_per = (tiles_max + owners - 1) // owners
    zero_index = jnp.zeros((), jnp.int32)
    tile_lanes = jnp.arange(tiles_max, dtype=jnp.int32)
    places = jnp.arange(slots_per, dtype=jnp.int32)
    tile_stack = weights.reshape(tiles_max * piece_len, block_len)

    def column_of(lookup):
        return lax.dynamic_index_in_dim(lookup.reshape(owners, columns, -1), my_column, 1, False)

    col_group = column_of(src_group)
    col_sub = column_of(src_sub)
    col_delay = column_of(delays)
    col_count = column_of(counts)[:, 0]
    matched = (col_group == my_group) & (tile_lanes[None, :] < col_count[:, None])
    ranked = jnp.cumsum(matched.astype(jnp.int32), axis=1) - 1
    picked_slot = matched[:, :, None] & (ranked[:, :, None] == places[None, None, :])
    sel_sub = jnp.sum(jnp.where(picked_slot, col_sub[:, :, None], 0), axis=1)
    sel_delay = jnp.sum(jnp.where(picked_slot, col_delay[:, :, None], 0), axis=1)
    own_group = lax.dynamic_index_in_dim(src_group, myself, 0, False)
    own_count = lax.dynamic_index_in_dim(counts, myself, 0, False)
    own_live = tile_lanes < own_count
    earlier = (
        (own_group[:, None] == own_group[None, :])
        & own_live[None, :]
        & (tile_lanes[None, :] < tile_lanes[:, None])
    )
    own_rank = jnp.minimum(jnp.sum(earlier.astype(jnp.int32), axis=1), slots_per - 1)
    own_mask = own_live.astype(jnp.bfloat16)

    def pack(cycle, in_times):
        how_many = in_times.shape[0]
        slot_ids = jnp.mod(in_times[None, :, None] - sel_delay[:, None, :], cycle_len)
        starts = jnp.broadcast_to(sel_sub[:, None, :] * piece_len, slot_ids.shape)

        def cut_piece(slot_id, start_id):
            return lax.dynamic_slice(
                cycle, (slot_id, zero_index, start_id), (1, replicas, piece_len)
            )[0]

        pieces = jax.vmap(cut_piece)(slot_ids.reshape(-1), starts.reshape(-1))
        return pieces.reshape(owners, how_many, slots_per, replicas, piece_len)

    def unpack(parcel):
        how_many = parcel.shape[1]
        picked = parcel[own_group, :, own_rank] * own_mask[:, None, None, None]
        flattened = jnp.transpose(picked, (1, 2, 0, 3)).reshape(
            how_many * replicas, tiles_max * piece_len
        )
        return jnp.dot(flattened, tile_stack, preferred_element_type=jnp.float32).reshape(
            how_many, replicas, block_len
        )

    def store_fire(cycle, population_variables, step_id):
        spike_density_result = sigmoid_spike_density(
            population_variables[1] - population_variables[2]
        ).astype(jnp.bfloat16)
        return lax.dynamic_update_slice(
            cycle, spike_density_result[None], (jnp.mod(step_id, cycle_len), zero_index, zero_index)
        )

    def record(sensors, population_variables, step_id):
        potential = (population_variables[1] - population_variables[2]).astype(jnp.bfloat16)
        local_sum = lax.dot_general(
            lead_field, potential, (((1,), (1,)), ((), ())), preferred_element_type=jnp.float32
        )
        local_sum = lax.psum(local_sum, ("grp", "node"))
        return lax.dynamic_update_slice(sensors, local_sum[None], (step_id, zero_index, zero_index))

    start_times = jnp.zeros((1,), jnp.int32)
    network_afferent = unpack(
        lax.all_to_all(pack(history, start_times), "grp", split_axis=0, concat_axis=0, tiled=True)
    )[0]
    sensors = jnp.zeros((STEPS, lead_field.shape[0], replicas), jnp.float32)

    def one_batch(batch_id, carried):
        population_variables, cycle, coupled_now, sensors = carried
        base_step = (jnp.asarray(batch_id) * DMIN).astype(jnp.int32)
        cycle = store_fire(cycle, population_variables, base_step)
        in_times = base_step + 1 + jnp.arange(DMIN, dtype=jnp.int32)
        batch_input = unpack(
            lax.all_to_all(pack(cycle, in_times), "grp", split_axis=0, concat_axis=0, tiled=True)
        )
        for offset in range(DMIN):
            step_id = base_step + offset
            if offset > 0:
                cycle = store_fire(cycle, population_variables, step_id)
            population_variables = advance(
                population_variables, afferent_noise_level, coupled_now, batch_input[offset]
            )
            coupled_now = batch_input[offset]
            sensors = record(sensors, population_variables, step_id)
        return (population_variables, cycle, coupled_now, sensors)

    population_variables, cycle, network_afferent, sensors = lax.fori_loop(
        0, STEPS // DMIN, one_batch, (initial, history, network_afferent, sensors)
    )
    return (population_variables, sensors)


def solution(mesh):
    return jax.shard_map(
        body,
        mesh=mesh,
        in_specs=(
            P(None, None, ("grp", "node")),
            P(None, ("grp", "node")),
            P(None, None, ("grp", "node")),
            P(("grp", "node"), None, None, None),
            P(None, ("grp", "node")),
            P(),
            P(),
            P(),
            P(),
        ),
        out_specs=(P(None, None, ("grp", "node")), P()),
        check_vma=False,
    )
```

profile of v0, /device:TPU:0, one launch (start us, length us, event | category | flops | bytes accessed | tf_op | source)
XLA Modules:
  0.0 292.0 jit_solution(6723610397220661307)
XLA Ops:
  7.2 0.8 reshape.515
  8.0 0.8 copy.46
  8.7 0.8 copy.44
  9.5 0.8 copy.43
  11.3 23.1 %copy.48 = bf16[64,32,1024]{1,0,2:T(8,128)(2,1)} copy(bf16[64,32,1024]{2,1,0:T(8,128)(2,1)} %param.11) | data formatting | bytes 8388608 | tf_op args[2]
  34.4 5.0 %gather_fusion = bf16[24,32,128]{1,0,2:T(8,128)(2,1)S(1)} fusion(bf16[64,32,1024]{1,0,2:T(8,128)(2,1)} %copy.48, s32[24]{0:T(128)S(1)} %fusion.184), kind=kCustom, calls=%fused_computation | custom fusion | bytes 393504 | tf_op jit(solution)/shard_map/vmap()/gather | solution.py:130
  39.5 1.1 copy.49
  40.6 7.3 %all-to-all-start = ((bf16[8,1,3,32,128]{4,3,2,1,0:T(8,128)(2,1)}), bf16[8,1,3,32,128]{4,3,2,1,0:T(8,128)(2,1)S(1)}, u32[]{:S(2)}, u32[]{:S(2)}) async-start(bf16[8,1,3,32,128]{4,3,2,1,0:T(8,128)(2,1)} %bitcast.8), calls=%async_computation | async-start | bytes 393216 | tf_op jit(solution)/shard_map/all_to_all | solution.py:165
  48.8 14.6 %dynamic_update_slice.38 = bf16[64,32,1024]{1,0,2:T(8,128)(2,1)} dynamic-update-slice(bf16[64,32,1024]{1,0,2:T(8,128)(2,1)} %copy.48, bf16[1,32,1024]{1,0,2:T(2,128)(2,1)S(1)} %copy.52, s32[]{:T(128)} %constant.159.clone.1, s32[]{:T(128)} %constant.159.clone.1, s32[]{:T(128)} %constant.159.clone.1) | dynamic-update-slice | bytes 131076 | tf_op jit(solution)/shard_map/while/body/eval_jaxpr/dynamic_update_slice | solution.py:151
  63.4 33.1 %gather_fusion.2 = bf16[144,32,128]{1,0,2:T(8,128)(2,1)} fusion(bf16[64,32,1024]{1,0,2:T(8,128)(2,1)} %dynamic_update_slice.38, s32[144]{0:T(256)S(1)} %bitcast.352), kind=kCustom, calls=%fused_computation.2 | custom fusion | bytes 2361024 | tf_op jit(solution)/shard_map/while/body/eval_jaxpr/vmap()/gather | solution.py:130
  96.5 7.6 %copy.55 = bf16[144,32,128]{2,1,0:T(8,128)(2,1)} copy(bf16[144,32,128]{1,0,2:T(8,128)(2,1)} %gather_fusion.2) | data formatting | bytes 2359296 | tf_op jit(solution)/shard_map/while/body/eval_jaxpr/vmap()/gather | solution.py:130
  104.1 6.1 %all-to-all-start.1 = ((bf16[8,6,3,32,128]{4,3,2,1,0:T(8,128)(2,1)}), bf16[8,6,3,32,128]{4,3,2,1,0:T(8,128)(2,1)}, u32[]{:S(2)}, u32[]{:S(2)}) async-start(bf16[8,6,3,32,128]{4,3,2,1,0:T(8,128)(2,1)} %bitcast.23), calls=%async_computation.1 | async-start | bytes 2359296 | tf_op jit(solution)/shard_map/while/body/eval_jaxpr/all_to_all | solution.py:175
  113.3 4.0 %fusion.23 = f32[1,32,1024]{2,1,0:T(8,128)S(1)} fusion(bf16[1,24,128,1024]{3,2,1,0:T(8,128)(2,1)} %param.12, bf16[24,32,128]{2,1,0:T(8,128)(2,1)S(1)} %gather_fusion.1, f32[32,1024]{1,0:T(8,128)S(1)} %copy-done.1, f32[6,32,1024]{2,1,0:T(8,128)S(1)} %copy-done.2, bf16[24]{0:T(256)(128)(2,1)S(1)} %fusion.185), kind=kOutput, calls=%fused_computation.16 | convolution fusion | flops 201883648 | bytes 7143472 | tf_op jit(solution)/shard_map/dot_general | solution.py:143
  118.8 0.8 fusion.129
  119.6 19.2 %all-to-all-done.1 = bf16[8,6,3,32,128]{4,3,2,1,0:T(8,128)(2,1)} async-done(((bf16[8,6,3,32,128]{4,3,2,1,0:T(8,128)(2,1)}), bf16[8,6,3,32,128]{4,3,2,1,0:T(8,128)(2,1)}, u32[]{:S(2)}, u32[]{:S(2)}) %all-to-all-start.1) | async-done | bytes 1179680 | tf_op jit(solution)/shard_map/while/body/eval_jaxpr/all_to_all | solution.py:175
  138.8 2.1 gather_fusion.3
  141.9 4.2 %fusion.2 = f32[192,1024]{1,0:T(8,128)S(1)} fusion(bf16[3072,1024]{1,0:T(8,128)(2,1)} %bitcast.351, bf16[24,8,24,128]{3,2,1,0:T(8,128)(2,1)S(1)} %bitcast.353), kind=kOutput, calls=%fused_computation.6 | convolution fusion | flops 1207959552 | bytes 8257536 | tf_op jit(solution)/shard_map/while/body/eval_jaxpr/dot_general | solution.py:143
  147.2 0.8 convolution_bitcast_fusion.5
  148.2 0.8 convolution_bitcast_fusion.4
  149.9 0.8 convolution_bitcast_fusion.3
  151.5 0.8 convolution_bitcast_fusion.2
  153.2 0.8 convolution_bitcast_fusion.1
  154.8 0.8 convolution_bitcast_fusion
  155.7 124.4 %all-reduce.4.cloned.1.call-done = (f32[1,128,32]{1,2,0:T(8,128)}, f32[1,128,32]{1,2,0:T(8,128)}, f32[1,128,32]{1,2,0:T(8,128)}, f32[1,128,32]{1,2,0:T(8,128)}, ...) async-done(((f32[1,128,32]{1,2,0:T(8,128)}, f32[1,128,32]{1,2,0:T(8,128)}, f32[1,128,32]{1,2,0:T(8,128)}, f32[1,128,32]{1,2,0:T(8,128)}, f32[1,128,32]{1,2,0:T(8,128)}, ...) | async-done | bytes 98320 | tf_op jit(solution)/shard_map/while/body/eval_jaxpr/psum | solution.py:160
  (118 shorter events, 16.6 us)
Async XLA Ops:
  7.2 140.0 %copy-start = (bf16[128,1024]{1,0:T(8,128)(2,1)S(1)}, bf16[128,1024]{1,0:T(8,128)(2,1)}, u32[]{:S(2)}) copy-start(bf16[128,1024]{1,0:T(8,128)(2,1)} %param.13) | copy-start | bytes 786436
  39.5 8.8 %copy-start.2 = (f32[6,32,1024]{2,1,0:T(8,128)S(1)}, f32[6,32,1024]{2,1,0:T(8,128)}, u32[]{:S(2)}) copy-start(f32[6,32,1024]{2,1,0:T(8,128)} %param.9) | copy-start | bytes 2359300
  40.6 63.5 %all-to-all-start = ((bf16[8,1,3,32,128]{4,3,2,1,0:T(8,128)(2,1)}), bf16[8,1,3,32,128]{4,3,2,1,0:T(8,128)(2,1)S(1)}, u32[]{:S(2)}, u32[]{:S(2)}) async-start(bf16[8,1,3,32,128]{4,3,2,1,0:T(8,128)(2,1)} %bitcast.8), calls=%async_computation | async-start | bytes 393216 | tf_op jit(solution)/shard_map/all_to_all | solution.py:165
  48.4 69.0 %copy-start.4 = (f32[1,32,1024]{2,1,0:T(8,128)}, f32[1,32,1024]{2,1,0:T(8,128)S(1)}, u32[]{:S(2)}) copy-start(f32[1,32,1024]{2,1,0:T(8,128)S(1)} %get-tuple-element.77) | copy-start | bytes 393220
  48.4 69.0 %copy-start.6 = (f32[1,32,1024]{2,1,0:T(8,128)}, f32[1,32,1024]{2,1,0:T(8,128)S(1)}, u32[]{:S(2)}) copy-start(f32[1,32,1024]{2,1,0:T(8,128)S(1)} %get-tuple-element.78) | copy-start | bytes 393220
  104.1 6.2 %copy-start.15 = (s32[32]{0:T(128)S(1)}, s32[32]{0:T(128)}, u32[]{:S(2)}) copy-start(s32[32]{0:T(128)} %param.17) | copy-start | bytes 388
  104.1 6.8 %copy-start.14 = (s32[32,24]{0,1:T(8,128)S(1)}, s32[32,24]{0,1:T(8,128)}, u32[]{:S(2)}) copy-start(s32[32,24]{0,1:T(8,128)} %param.14) | copy-start | bytes 9220
  104.1 34.8 %all-to-all-start.1 = ((bf16[8,6,3,32,128]{4,3,2,1,0:T(8,128)(2,1)}), bf16[8,6,3,32,128]{4,3,2,1,0:T(8,128)(2,1)}, u32[]{:S(2)}, u32[]{:S(2)}) async-start(bf16[8,6,3,32,128]{4,3,2,1,0:T(8,128)(2,1)} %bitcast.23), calls=%async_computation.1 | async-start | bytes 2359296 | tf_op jit(solution)/shard_map/while/body/eval_jaxpr/all_to_all | solution.py:175
  110.2 3.1 %copy-start.1 = (f32[32,1024]{1,0:T(8,128)S(1)}, f32[32,1024]{1,0:T(8,128)}, u32[]{:S(2)}) copy-start(f32[32,1024]{1,0:T(8,128)} %param.10) | copy-start | bytes 393220
  110.2 169.9 %all-reduce.4.cloned.1.call-start = ((), (), s32[]{:S(2)}) async-start(), calls=%async_computation.2 | async-start | bytes 196608 | tf_op jit(solution)/shard_map/while/body/eval_jaxpr/psum | solution.py:160
  117.4 0.7 copy-start.8
  141.9 4.4 %copy-start.3 = (f32[3,32,1024]{2,1,0:T(8,128)S(1)}, f32[3,32,1024]{2,1,0:T(8,128)}, u32[]{:S(2)}) copy-start(f32[3,32,1024]{2,1,0:T(8,128)} %slice.528) | copy-start | bytes 1179652
  141.9 4.4 %copy-start.5 = (f32[1,32,1024]{2,1,0:T(8,128)S(1)}, f32[1,32,1024]{2,1,0:T(8,128)}, u32[]{:S(2)}) copy-start(f32[1,32,1024]{2,1,0:T(8,128)} %copy-done.4) | copy-start | bytes 393220
  141.9 4.4 %copy-start.7 = (f32[1,32,1024]{2,1,0:T(8,128)S(1)}, f32[1,32,1024]{2,1,0:T(8,128)}, u32[]{:S(2)}) copy-start(f32[1,32,1024]{2,1,0:T(8,128)} %copy-done.6) | copy-start | bytes 393220
  141.9 4.4 %copy-start.9 = (f32[1,32,1024]{2,1,0:T(8,128)S(1)}, f32[1,32,1024]{2,1,0:T(8,128)}, u32[]{:S(2)}) copy-start(f32[1,32,1024]{2,1,0:T(8,128)} %copy-done.8) | copy-start | bytes 393220
  141.9 4.4 %copy-start.11 = (f32[1,32,1024]{2,1,0:T(8,128)S(1)}, f32[1,32,1024]{2,1,0:T(8,128)}, u32[]{:S(2)}) copy-start(f32[1,32,1024]{2,1,0:T(8,128)} %get-tuple-element.74) | copy-start | bytes 393220
  141.9 4.4 %copy-start.12 = (f32[1,32,1024]{2,1,0:T(8,128)S(1)}, f32[1,32,1024]{2,1,0:T(8,128)}, u32[]{:S(2)}) copy-start(f32[1,32,1024]{2,1,0:T(8,128)} %get-tuple-element.75) | copy-start | bytes 393220
  154.8 129.6 %copy-start.10 = (f32[6,32,1024]{2,1,0:T(8,128)}, f32[6,32,1024]{2,1,0:T(8,128)S(1)}, u32[]{:S(2)}) copy-start(f32[6,32,1024]{2,1,0:T(8,128)S(1)} %fusion.37) | copy-start | bytes 2359300
  284.5 0.6 copy-start.13
Sparse Core Ops, SparseCore 0:
  155.8 124.2 all-reduce.3
where the time goes:
time: 294 us; the launch traced here: 292 us
  waiting for transfers between devices  144 us (49%)
  local copies, waits for them, and re-layouts  99.7 us (34%)
  between operations  14.7 us (5%)
  starting transfers between devices  13.4 us (5%)
  matrix products  13.1 us (4%)
  other arithmetic  7.27 us (2%)
    psum x1, waiting for transfers between devices, record(): local_sum = lax.psum(local_sum, ('grp', 'node'))  124 us
    gather x4, local copies, waits for them, and re-layouts, cut_piece(): lax.dynamic_slice(cycle, (slot_id, zero_index, start_id), (1, replicas, p...  46.8 us
    unnamed x36, local copies, waits for them, and re-layouts  26.6 us
    all_to_all x1, waiting for transfers between devices, one_batch(): lax.all_to_all(pack(cycle, in_times), 'grp', split_axis=0, concat_axis=0,...  19.2 us
    dynamic_update_slice x1, local copies, waits for them, and re-layouts, store_fire(): lax.dynamic_update_slice(cycle, spike_density_result[None], (jnp.mod(step...  14.6 us
    dot_general x2, matrix products, unpack(): jnp.dot(flattened, tile_stack, preferred_element_type=jnp.float32)  8.29 us
    all_to_all x1, starting transfers between devices, body(): lax.all_to_all(pack(history, start_times), 'grp', split_axis=0, concat_ax...  7.26 us
    all_to_all x1, starting transfers between devices, one_batch(): lax.all_to_all(pack(cycle, in_times), 'grp', split_axis=0, concat_axis=0,...  6.14 us
  transfers between devices with their start and end apart: 3, of which 2 were waited for; matrix products, arithmetic and copies ran while one was open for 22% of the time, Pallas kernels for 0%

commit v1 on v0

v1 whole, which is shorter than its diff:
```python
import functools

import jax
import jax.numpy as jnp
from jax import lax
from jax.experimental import pallas as pl
from jax.experimental.pallas import tpu as pltpu
from jax.sharding import PartitionSpec as P

DMIN = 6
STEPS = 6
TIME_GROUPS = ((0, 1), (2, 3), (4, 5), (6,))

exciting_amplitude = 3.25
suppressive_amplitude = 22.0
exciting_inverse_lag = 0.1
suppressive_inverse_lag = 0.05
link_factor = 135.0
maximal_spike_frequency = 0.005
thresh = 6.0
fire_slope = 0.56
global_scaling_factor = 0.5
dt_step = 0.5

MESH = pl.DeviceIdType.MESH


def sigmoid_spike_density(level):
    return 1.0 / (1.0 + jnp.exp(fire_slope * (thresh - level)))


def derivative(y, noise, coupled):
    curvature = (
        exciting_amplitude
        * exciting_inverse_lag
        * maximal_spike_frequency
        * sigmoid_spike_density(y[1] - y[2])
        - 2.0 * exciting_inverse_lag * y[3]
        - exciting_inverse_lag * exciting_inverse_lag * y[0]
    )
    interneuron = (
        exciting_amplitude
        * exciting_inverse_lag
        * (
            noise
            + 0.8
            * link_factor
            * maximal_spike_frequency
            * sigmoid_spike_density(link_factor * y[0])
            + global_scaling_factor * coupled
        )
        - 2.0 * exciting_inverse_lag * y[4]
        - exciting_inverse_lag * exciting_inverse_lag * y[1]
    )
    suppressive = (
        suppressive_amplitude
        * suppressive_inverse_lag
        * 0.25
        * link_factor
        * maximal_spike_frequency
        * sigmoid_spike_density(0.25 * link_factor * y[0])
        - 2.0 * suppressive_inverse_lag * y[5]
        - suppressive_inverse_lag * suppressive_inverse_lag * y[2]
    )
    return [y[3], y[4], y[5], curvature, interneuron, suppressive]


def advance(y, noise, coupled_now, coupled_next):
    first = derivative(y, noise, coupled_now)
    moved = [a + dt_step * b for a, b in zip(y, first)]
    second = derivative(moved, noise, coupled_next)
    return [a + 0.5 * dt_step * (b + c) for a, b, c in zip(y, first, second)]


def pack_kernel(
    owners,
    columns,
    slots,
    src_group,
    src_sub,
    delays,
    counts,
    initial,
    hist,
    own_place,
    *rest,
):
    groups = len(TIME_GROUPS)
    packed = rest[:groups]
    sel_sub, sel_delay, fired = rest[groups:]
    me = lax.axis_index("grp")
    column = lax.axis_index("node")
    cycle_len, replicas, block_len = hist.shape
    tiles = src_group.shape[0]
    piece_len = packed[0].shape[3]

    def choose(dest, carry):
        block = dest * columns + column
        live = counts[block]
        rank = jnp.int32(0)
        subs = [jnp.int32(0)] * slots
        waits = [jnp.int32(DMIN)] * slots
        for k in range(tiles):
            hit = jnp.logical_and(src_group[k, block] == me, k < live)
            sub, wait = src_sub[k, block], delays[k, block]
            for r in range(slots):
                take = jnp.logical_and(hit, rank == r)
                subs[r] = jnp.where(take, sub, subs[r])
                waits[r] = jnp.where(take, wait, waits[r])
            rank = rank + jnp.where(hit, 1, 0)
        for r in range(slots):
            sel_sub[dest * slots + r] = subs[r]
            sel_delay[dest * slots + r] = waits[r]
        return carry

    lax.fori_loop(0, owners, choose, 0)

    my_block = me * columns + column
    my_live = counts[my_block]
    my_groups = [src_group[k, my_block] for k in range(tiles)]
    for k in range(tiles):
        rank = jnp.int32(0)
        for earlier in range(k):
            rank = rank + jnp.where(my_groups[earlier] == my_groups[k], 1, 0)
        place = my_groups[k] * slots + jnp.minimum(rank, slots - 1)
        own_place[k] = jnp.where(k < my_live, place, owners * slots)

    def first_fire(tile, carry):
        cols = pl.ds(pl.multiple_of(tile * piece_len, piece_len), piece_len)
        fire = sigmoid_spike_density(initial[1, :, cols] - initial[2, :, cols])
        fired[:, cols] = fire.astype(jnp.bfloat16)
        return carry

    lax.fori_loop(0, block_len // piece_len, first_fire, 0)

    def pack(place, carry):
        start = cycle_len - sel_delay[place]
        cols = pl.ds(pl.multiple_of(sel_sub[place] * piece_len, piece_len), piece_len)
        for times, parcel in zip(TIME_GROUPS, packed):
            for j, t in enumerate(times):
                if t < DMIN:
                    parcel[place, j] = hist[start + t, :, cols]
                else:
                    past = hist[jnp.minimum(start + t, cycle_len - 1), :, cols]
                    parcel[place, j] = jnp.where(start + t < cycle_len, past, fired[:, cols])
        return carry

    lax.fori_loop(0, owners * slots, pack, 0)


def kernel(
    owners,
    columns,
    slots,
    own_place,
    initial,
    noise,
    weights,
    lead,
    *rest,
):
    group_count = len(TIME_GROUPS)
    packed = rest[:group_count]
    landed = rest[-group_count:]
    run(owners, columns, slots, own_place, initial, noise, weights, lead, packed, landed, *rest[group_count:-group_count])


def run(
    owners,
    columns,
    slots,
    own_place,
    initial,
    noise,
    weights,
    lead,
    packed,
    landed,
    state,
    sensors_out,
    lhs,
    coupled,
    potential,
    partial,
    scatter_in,
    node_in,
    gathered,
    send_sem,
    recv_sem,
    scatter_send,
    scatter_recv,
    node_send,
    node_recv,
    gather_send,
    gather_recv,
):
    group_count = len(TIME_GROUPS)
    me = lax.axis_index("grp")
    column = lax.axis_index("node")
    replicas, block_len = noise.shape
    tiles = own_place.shape[0]
    piece_len = weights.shape[0] // tiles
    offsets = sorted(range(1, owners), key=lambda o: abs(2 * o - owners))

    barrier = pltpu.get_barrier_semaphore()
    for o in offsets:
        pl.semaphore_signal(
            barrier, inc=1, device_id={"grp": lax.rem(me + o, owners)}, device_id_type=MESH
        )
    for o in range(1, columns):
        pl.semaphore_signal(
            barrier, inc=1, device_id={"node": lax.rem(column + o, columns)}, device_id_type=MESH
        )

    mine = pl.ds(me * slots, slots)
    spare = owners * slots
    for g in range(group_count):
        landed[g][mine] = packed[g][mine]
        landed[g][spare] = jnp.zeros(landed[g].shape[1:], jnp.bfloat16)

    pl.semaphore_wait(barrier, owners + columns - 2)

    def parcel_copy(g, o):
        dest = lax.rem(me + o, owners)
        return pltpu.make_async_remote_copy(
            src_ref=packed[g].at[pl.ds(dest * slots, slots)],
            dst_ref=landed[g].at[mine],
            send_sem=send_sem.at[g, o],
            recv_sem=recv_sem.at[g, o],
            device_id={"grp": dest},
            device_id_type=MESH,
        )

    for g in range(group_count):
        for o in offsets:
            parcel_copy(g, o).start()

    dot_cols = min(256, block_len)
    rows_per = replicas
    chunk = partial.shape[1]

    for g, times in enumerate(TIME_GROUPS):
        for o in offsets:
            parcel_copy(g, o).wait_recv()
        rows = len(times) * rows_per
        base = times[0] * rows_per

        for k in range(tiles):
            piece = landed[g][own_place[k]]
            lhs[:rows, k * piece_len : (k + 1) * piece_len] = piece.reshape(rows, piece_len)

        def multiply(tile, carry):
            cols = pl.ds(pl.multiple_of(tile * dot_cols, dot_cols), dot_cols)
            coupled[base : base + rows, cols] = jnp.dot(
                lhs[:rows, :], weights[:, cols], preferred_element_type=jnp.float32
            )
            return carry

        lax.fori_loop(0, block_len // dot_cols, multiply, 0)

        steps = [t - 1 for t in times if t > 0]

        source = initial if g == 0 else state

        def move(tile, carry):
            cols = pl.ds(pl.multiple_of(tile * piece_len, piece_len), piece_len)
            y = [source[i, :, cols] for i in range(6)]
            drive = noise[:, cols]
            now = coupled[steps[0] * rows_per : (steps[0] + 1) * rows_per, cols]
            for i, s in enumerate(steps):
                later = coupled[(s + 1) * rows_per : (s + 2) * rows_per, cols]
                y = advance(y, drive, now, later)
                now = later
                potential[i * rows_per : (i + 1) * rows_per, cols] = (y[1] - y[2]).astype(
                    jnp.bfloat16
                )
            for i in range(6):
                state[i, :, cols] = y[i]
            return carry

        lax.fori_loop(0, block_len // piece_len, move, 0)

        signal = lax.dot_general(
            potential[: len(steps) * rows_per, :],
            lead[...],
            (((1,), (1,)), ((), ())),
            preferred_element_type=jnp.float32,
        )
        row = steps[0] * rows_per
        stop = row + len(steps) * rows_per
        first_row = row
        while row < stop:
            part, inside = divmod(row, chunk)
            many = min(chunk - inside, stop - row)
            partial[part, inside : inside + many, :] = signal[
                row - first_row : row - first_row + many, :
            ]
            row += many

    def scatter_copy(o):
        dest = lax.rem(me + o, owners)
        return pltpu.make_async_remote_copy(
            src_ref=partial.at[dest],
            dst_ref=scatter_in.at[o],
            send_sem=scatter_send.at[o],
            recv_sem=scatter_recv.at[o],
            device_id={"grp": dest},
            device_id_type=MESH,
        )

    for o in offsets:
        scatter_copy(o).start()
    for g in range(group_count):
        for o in offsets:
            parcel_copy(g, o).wait_send()
    total = partial[me]
    for o in reversed(offsets):
        scatter_copy(o).wait_recv()
        total = total + scatter_in[o]
    node_in[column] = total

    def node_copy(o):
        return pltpu.make_async_remote_copy(
            src_ref=node_in.at[column],
            dst_ref=node_in.at[column],
            send_sem=node_send.at[o],
            recv_sem=node_recv.at[o],
            device_id={"node": lax.rem(column + o, columns)},
            device_id_type=MESH,
        )

    for o in range(1, columns):
        node_copy(o).start()
    for o in range(1, columns):
        node_copy(o).wait_recv()
    total = node_in[0]
    for c in range(1, columns):
        total = total + node_in[c]
    gathered[me] = total

    def gather_copy(o):
        return pltpu.make_async_remote_copy(
            src_ref=gathered.at[me],
            dst_ref=gathered.at[me],
            send_sem=gather_send.at[o],
            recv_sem=gather_recv.at[o],
            device_id={"grp": lax.rem(me + o, owners)},
            device_id_type=MESH,
        )

    for o in offsets:
        gather_copy(o).start()
    for o in offsets:
        scatter_copy(o).wait_send()
    for o in range(1, columns):
        node_copy(o).wait_send()
    for o in offsets:
        gather_copy(o).wait_recv()
    sensors_out[...] = gathered[...]
    for o in offsets:
        gather_copy(o).wait_send()


def body(
    owners,
    columns,
    initial,
    afferent_noise_level,
    history,
    weights,
    lead_field,
    src_group,
    src_sub,
    delays,
    counts,
):
    cycle_len, replicas, block_len = history.shape
    tiles = src_group.shape[1]
    piece_len = weights.shape[2]
    sensors = lead_field.shape[0]
    slots = (tiles + owners - 1) // owners
    chunk = (STEPS * replicas + owners - 1) // owners
    groups = len(TIME_GROUPS)
    most = max(len(times) for times in TIME_GROUPS) * replicas
    smem = pl.BlockSpec(memory_space=pltpu.SMEM)
    vmem = pl.BlockSpec(memory_space=pltpu.VMEM)
    own_place, *packed = pl.pallas_call(
        functools.partial(pack_kernel, owners, columns, slots),
        out_shape=[jax.ShapeDtypeStruct((tiles,), jnp.int32)]
        + [
            jax.ShapeDtypeStruct(
                (owners * slots, len(times), replicas, piece_len), jnp.bfloat16
            )
            for times in TIME_GROUPS
        ],
        in_specs=[smem] * 4 + [vmem] * 2,
        out_specs=[smem] + [vmem] * groups,
        scratch_shapes=[
            pltpu.SMEM((owners * slots,), jnp.int32),
            pltpu.SMEM((owners * slots,), jnp.int32),
            pltpu.VMEM((replicas, block_len), jnp.bfloat16),
        ],
        compiler_params=pltpu.CompilerParams(vmem_limit_bytes=8 * 1024 * 1024),
        cost_estimate=pl.CostEstimate(flops=0, bytes_accessed=8 * 1024 * 1024, transcendentals=0),
    )(src_group.T, src_sub.T, delays.T, counts, initial, history)
    final, signal = pl.pallas_call(
        functools.partial(kernel, owners, columns, slots),
        out_shape=(
            jax.ShapeDtypeStruct(initial.shape, jnp.float32),
            jax.ShapeDtypeStruct((owners, chunk, sensors), jnp.float32),
        ),
        in_specs=[smem] + [vmem] * (4 + groups),
        out_specs=(vmem, vmem),
        scratch_shapes=[
            pltpu.VMEM((most, tiles * piece_len), jnp.bfloat16),
            pltpu.VMEM(((STEPS + 1) * replicas, block_len), jnp.float32),
            pltpu.VMEM((most, block_len), jnp.bfloat16),
            pltpu.VMEM((owners, chunk, sensors), jnp.float32),
            pltpu.VMEM((owners, chunk, sensors), jnp.float32),
            pltpu.VMEM((columns, chunk, sensors), jnp.float32),
            pltpu.VMEM((owners, chunk, sensors), jnp.float32),
            pltpu.SemaphoreType.DMA((groups, owners)),
            pltpu.SemaphoreType.DMA((groups, owners)),
            pltpu.SemaphoreType.DMA((owners,)),
            pltpu.SemaphoreType.DMA((owners,)),
            pltpu.SemaphoreType.DMA((columns,)),
            pltpu.SemaphoreType.DMA((columns,)),
            pltpu.SemaphoreType.DMA((owners,)),
            pltpu.SemaphoreType.DMA((owners,)),
        ]
        + [
            pltpu.VMEM((owners * slots + 1, len(times), replicas, piece_len), jnp.bfloat16)
            for times in TIME_GROUPS
        ],
        compiler_params=pltpu.CompilerParams(
            collective_id=0, has_side_effects=True, vmem_limit_bytes=20 * 1024 * 1024
        ),
    )(
        own_place,
        initial,
        afferent_noise_level,
        weights.reshape(tiles * piece_len, block_len),
        lead_field,
        *packed,
    )
    signal = signal.reshape(owners * chunk, sensors)[: STEPS * replicas]
    signal = signal.reshape(STEPS, replicas, sensors)
    return final, jnp.transpose(signal, (0, 2, 1))


def solution(mesh):
    return jax.shard_map(
        functools.partial(body, mesh.shape["grp"], mesh.shape["node"]),
        mesh=mesh,
        in_specs=(
            P(None, None, ("grp", "node")),
            P(None, ("grp", "node")),
            P(None, None, ("grp", "node")),
            P(("grp", "node"), None, None, None),
            P(None, ("grp", "node")),
            P(),
            P(),
            P(),
            P(),
        ),
        out_specs=(P(None, None, ("grp", "node")), P()),
        check_vma=False,
    )
```

time: 294 us -> 72.3 us (0.25)
  waiting for transfers between devices: 144 us -> 0 us
  local copies, waits for them, and re-layouts: 99.7 us -> 13.4 us
  Pallas kernels: 0 us -> 57.8 us
  between operations: 14.7 us -> 0.67 us
  starting transfers between devices: 13.4 us -> 0 us
  matrix products: 13.1 us -> 0 us
  other arithmetic: 7.27 us -> 0 us
    psum x1 -> x0, waiting for transfers between devices: 124 us -> none  [record(): local_sum = lax.psum(local_sum, ('grp', 'node'))]
    pallas_call x0 -> x2, Pallas kernels: none -> 57.8 us  [the longest x1 53.6 us: body(): pl.pallas_call(functools.partial(kernel, owners, columns, slots), out_sha...]
    gather x6 -> x0, local copies, waits for them, and re-layouts: 49.6 us -> none  [the longest x4 46.8 us: cut_piece(): lax.dynamic_slice(cycle, (slot_id, zero_index, start_id), (1, replicas, p...]
    all_to_all x2 -> x0, waiting for transfers between devices: 19.2 us -> none  [the longest x1 19.2 us: one_batch(): lax.all_to_all(pack(cycle, in_times), 'grp', split_axis=0, concat_axis=0,...]
    dynamic_update_slice x7 -> x0, local copies, waits for them, and re-layouts: 18.9 us -> none  [the longest x1 14.6 us: store_fire(): lax.dynamic_update_slice(cycle, spike_density_result[None], (jnp.mod(step...]
    all_to_all x2 -> x0, starting transfers between devices: 13.4 us -> none  [the longest x1 7.26 us: body(): lax.all_to_all(pack(history, start_times), 'grp', split_axis=0, concat_ax...]
    unnamed x36 -> x22, local copies, waits for them, and re-layouts: 26.6 us -> 13.4 us
    dot_general x8 -> x0, matrix products: 13.1 us -> none  [the longest x2 8.29 us: unpack(): jnp.dot(flattened, tile_stack, preferred_element_type=jnp.float32)]
  transfers between devices with their start and end apart: 3 -> 0, of which waited for: 2 -> 0; matrix products, arithmetic and copies ran while one was open for 22% -> 0% of each run, Pallas kernels for 0% -> 0%
where the time goes in v1:
time: 72.3 us; the launch traced here: 71.9 us
  Pallas kernels  57.8 us (80%)
  local copies, waits for them, and re-layouts  13.4 us (19%)
    pallas_call x1, Pallas kernels, body(): pl.pallas_call(functools.partial(kernel, owners, columns, slots), out_sha...  53.6 us
    unnamed x22, local copies, waits for them, and re-layouts  13.4 us
    pallas_call x1, Pallas kernels, body(): pl.pallas_call(functools.partial(pack_kernel, owners, columns, slots), ou...  4.18 us

profile of v1, /device:TPU:0, one launch (start us, length us, event | category | flops | bytes accessed | tf_op | source)
XLA Modules:
  0.0 71.9 jit_solution(13727069692014987701)
XLA Ops:
  0.6 0.0 copy-start.1
  0.6 2.2 %copy-done.1 = bf16[64,32,1024]{2,1,0:T(8,128)(2,1)S(1)} copy-done((bf16[64,32,1024]{2,1,0:T(8,128)(2,1)S(1)}, bf16[64,32,1024]{2,1,0:T(8,128)(2,1)}, u32[]{:S(2)}) %copy-start.1) | copy-done | bytes 4194328
  2.8 0.0 copy-start.2
  2.8 1.1 %copy-done.2 = f32[6,32,1024]{2,1,0:T(8,128)S(1)} copy-done((f32[6,32,1024]{2,1,0:T(8,128)S(1)}, f32[6,32,1024]{2,1,0:T(8,128)}, u32[]{:S(2)}) %copy-start.2) | copy-done | bytes 786456
  4.0 0.0 copy-start.6
  4.0 0.7 copy-done.6
  4.7 0.0 copy-start.7
  4.7 0.7 copy-done.7
  5.4 0.0 copy-start.8
  5.4 0.7 copy-done.8
  6.1 0.0 copy-start.9
  6.1 0.7 copy-done.9
  6.7 4.2 %shard_map.104 = (s32[24]{0:T(128)S(1)}, bf16[24,2,32,128]{3,2,1,0:T(8,128)(2,1)S(1)}, bf16[24,2,32,128]{3,2,1,0:T(8,128)(2,1)S(1)}, bf16[24,2,32,128]{3,2,1,0:T(8,128)(2,1)S(1)}, bf16[24,1,32,128]{3,2,1,0:T(8,128)(2,1)S(1)}) custom-call(s32[24,32]{1,0:T(8,128)S(1)} %bitcast.9, s32[24,32]{1,0:T(8,128)S(1)} %bitcast.10, s32[24,32]{1,0:T(8,128)S(1)} %bitcast.11, ...), custom_call_target="tpu_custom_call" | custom-call | bytes 8388608 | tf_op jit(solution)/shard_map/pallas_call | solution.py:387
  10.9 0.0 copy-start
  10.9 2.8 %copy-done = bf16[1,24,128,1024]{3,2,1,0:T(8,128)(2,1)S(1)} copy-done((bf16[1,24,128,1024]{3,2,1,0:T(8,128)(2,1)S(1)}, bf16[1,24,128,1024]{3,2,1,0:T(8,128)(2,1)}, u32[]{:S(2)}) %copy-start) | copy-done | bytes 6291480
  13.7 0.0 copy-start.3
  13.7 1.1 %copy-done.3 = f32[6,32,1024]{2,1,0:T(8,128)S(1)} copy-done((f32[6,32,1024]{2,1,0:T(8,128)S(1)}, f32[6,32,1024]{2,1,0:T(8,128)}, u32[]{:S(2)}) %copy-start.3) | copy-done | bytes 786456
  14.8 0.0 copy-start.4
  14.8 0.9 %copy-done.4 = bf16[128,1024]{1,0:T(8,128)(2,1)S(1)} copy-done((bf16[128,1024]{1,0:T(8,128)(2,1)S(1)}, bf16[128,1024]{1,0:T(8,128)(2,1)}, u32[]{:S(2)}) %copy-start.4) | copy-done | bytes 262168
  15.8 0.0 copy-start.5
  15.8 0.9 %copy-done.5 = f32[32,1024]{1,0:T(8,128)S(1)} copy-done((f32[32,1024]{1,0:T(8,128)S(1)}, f32[32,1024]{1,0:T(8,128)}, u32[]{:S(2)}) %copy-start.5) | copy-done | bytes 131096
  16.7 53.6 %shard_map.105 = (f32[6,32,1024]{2,1,0:T(8,128)S(1)}, f32[8,24,128]{2,1,0:T(8,128)S(1)}) custom-call(s32[24]{0:T(128)S(1)} %get-tuple-element.9.own_place, f32[6,32,1024]{2,1,0:T(8,128)S(1)} %copy-done.3, f32[32,1024]{1,0:T(8,128)S(1)} %copy-done.5, bf16[3072,1024]{1,0:T(8,128)(2,1)S(1)} %bitcast.7, bf16[128,1024]{1,0:T(8,128)(2,1)S(1)} %copy-done.4, ...), custom_call_target="tpu_custom_call" | custom-call | tf_op jit(solution)/shard_map/pallas_call | solution.py:406
  70.3 0.9 %copy.13 = f32[6,32,1024]{2,1,0:T(8,128)} copy(f32[6,32,1024]{2,1,0:T(8,128)S(1)} %get-tuple-element.18) | data formatting | bytes 1572864
  71.2 0.6 copy.14
Async XLA Ops:
  0.6 2.2 %copy-start.1 = (bf16[64,32,1024]{2,1,0:T(8,128)(2,1)S(1)}, bf16[64,32,1024]{2,1,0:T(8,128)(2,1)}, u32[]{:S(2)}) copy-start(bf16[64,32,1024]{2,1,0:T(8,128)(2,1)} %hist.1) | copy-start | bytes 12582916
  2.8 1.1 %copy-start.2 = (f32[6,32,1024]{2,1,0:T(8,128)S(1)}, f32[6,32,1024]{2,1,0:T(8,128)}, u32[]{:S(2)}) copy-start(f32[6,32,1024]{2,1,0:T(8,128)} %initial.3) | copy-start | bytes 2359300
  4.0 0.7 copy-start.6
  4.7 0.7 copy-start.7
  5.4 0.7 copy-start.8
  6.1 0.7 copy-start.9
  10.9 2.8 %copy-start = (bf16[1,24,128,1024]{3,2,1,0:T(8,128)(2,1)S(1)}, bf16[1,24,128,1024]{3,2,1,0:T(8,128)(2,1)}, u32[]{:S(2)}) copy-start(bf16[1,24,128,1024]{3,2,1,0:T(8,128)(2,1)} %param.12) | copy-start | bytes 18874372
  13.7 1.1 %copy-start.3 = (f32[6,32,1024]{2,1,0:T(8,128)S(1)}, f32[6,32,1024]{2,1,0:T(8,128)}, u32[]{:S(2)}) copy-start(f32[6,32,1024]{2,1,0:T(8,128)} %initial.3) | copy-start | bytes 2359300
  14.8 0.9 %copy-start.4 = (bf16[128,1024]{1,0:T(8,128)(2,1)S(1)}, bf16[128,1024]{1,0:T(8,128)(2,1)}, u32[]{:S(2)}) copy-start(bf16[128,1024]{1,0:T(8,128)(2,1)} %lead.1) | copy-start | bytes 786436
  15.8 0.9 %copy-start.5 = (f32[32,1024]{1,0:T(8,128)S(1)}, f32[32,1024]{1,0:T(8,128)}, u32[]{:S(2)}) copy-start(f32[32,1024]{1,0:T(8,128)} %noise.1) | copy-start | bytes 393220

commit v2 on v1

--- a/solution.py
+++ b/solution.py
@@ -9,6 +9,7 @@
 
 DMIN = 6
 STEPS = 6
+VMEM_BYTES = 67043328
 TIME_GROUPS = ((0, 1), (2, 3), (4, 5), (6,))
 
 exciting_amplitude = 3.25
@@ -80,19 +81,24 @@
     src_sub,
     delays,
     counts,
-    initial,
-    hist,
+    initial_hbm,
+    history_hbm,
     own_place,
     *rest,
 ):
     groups = len(TIME_GROUPS)
     packed = rest[:groups]
-    sel_sub, sel_delay, fired = rest[groups:]
+    sel_sub, sel_delay, fired, fields, hist, local_sem = rest[groups:]
     me = lax.axis_index("grp")
     column = lax.axis_index("node")
     cycle_len, replicas, block_len = hist.shape
     tiles = src_group.shape[0]
     piece_len = packed[0].shape[3]
+
+    load_fields = pltpu.make_async_copy(initial_hbm.at[pl.ds(1, 2)], fields, local_sem.at[0])
+    load_history = pltpu.make_async_copy(history_hbm, hist, local_sem.at[1])
+    load_fields.start()
+    load_history.start()
 
     def choose(dest, carry):
         block = dest * columns + column
@@ -125,13 +131,17 @@
         place = my_groups[k] * slots + jnp.minimum(rank, slots - 1)
         own_place[k] = jnp.where(k < my_live, place, owners * slots)
 
+    load_fields.wait()
+
     def first_fire(tile, carry):
         cols = pl.ds(pl.multiple_of(tile * piece_len, piece_len), piece_len)
-        fire = sigmoid_spike_density(initial[1, :, cols] - initial[2, :, cols])
+        fire = sigmoid_spike_density(fields[0, :, cols] - fields[1, :, cols])
         fired[:, cols] = fire.astype(jnp.bfloat16)
         return carry
 
     lax.fori_loop(0, block_len // piece_len, first_fire, 0)
+
+    load_history.wait()
 
     def pack(place, carry):
         start = cycle_len - sel_delay[place]
@@ -153,50 +163,50 @@
     columns,
     slots,
     own_place,
-    initial,
-    noise,
-    weights,
-    lead,
+    initial_hbm,
+    noise_hbm,
+    weights_hbm,
+    lead_hbm,
     *rest,
 ):
     group_count = len(TIME_GROUPS)
     packed = rest[:group_count]
     landed = rest[-group_count:]
-    run(owners, columns, slots, own_place, initial, noise, weights, lead, packed, landed, *rest[group_count:-group_count])
-
-
-def run(
-    owners,
-    columns,
-    slots,
-    own_place,
-    initial,
-    noise,
-    weights,
-    lead,
-    packed,
-    landed,
-    state,
-    sensors_out,
-    lhs,
-    coupled,
-    potential,
-    partial,
-    scatter_in,
-    node_in,
-    gathered,
-    send_sem,
-    recv_sem,
-    scatter_send,
-    scatter_recv,
-    node_send,
-    node_recv,
-    gather_send,
-    gather_recv,
-):
-    group_count = len(TIME_GROUPS)
+    staged = rest[-2 * group_count : -group_count]
+    (
+        final_hbm,
+        sensors_out,
+        state,
+        noise,
+        weights,
+        lead,
+        lhs,
+        coupled,
+        potential,
+        partial,
+        scatter_in,
+        node_in,
+        gathered,
+        local_sem,
+        keep_sem,
+        stage_sem,
+        send_sem,
+        recv_sem,
+        scatter_send,
+        scatter_recv,
+        node_send,
+        node_recv,
+        gather_send,
+        gather_recv,
+    ) = rest[group_count : -2 * group_count]
     me = lax.axis_index("grp")
     column = lax.axis_index("node")
+    mine = pl.ds(me * slots, slots)
+    stage = [
+        pltpu.make_async_copy(packed[g], staged[g], stage_sem.at[g]) for g in range(group_count)
+    ]
+    for copy in stage:
+        copy.start()
     replicas, block_len = noise.shape
     tiles = own_place.shape[0]
     piece_len = weights.shape[0] // tiles
@@ -212,18 +222,30 @@
             barrier, inc=1, device_id={"node": lax.rem(column + o, columns)}, device_id_type=MESH
         )
 
-    mine = pl.ds(me * slots, slots)
     spare = owners * slots
     for g in range(group_count):
-        landed[g][mine] = packed[g][mine]
         landed[g][spare] = jnp.zeros(landed[g].shape[1:], jnp.bfloat16)
 
+    for copy in stage:
+        copy.wait()
+    keep = [
+        pltpu.make_async_copy(packed[g].at[mine], landed[g].at[mine], keep_sem.at[g])
+        for g in range(group_count)
+    ]
+    loads = [
+        pltpu.make_async_copy(weights_hbm, weights, local_sem.at[0]),
+        pltpu.make_async_copy(initial_hbm, state, local_sem.at[1]),
+        pltpu.make_async_copy(noise_hbm, noise, local_sem.at[2]),
+        pltpu.make_async_copy(lead_hbm, lead, local_sem.at[3]),
+    ]
+    for copy in keep + loads:
+        copy.start()
     pl.semaphore_wait(barrier, owners + columns - 2)
 
     def parcel_copy(g, o):
         dest = lax.rem(me + o, owners)
         return pltpu.make_async_remote_copy(
-            src_ref=packed[g].at[pl.ds(dest * slots, slots)],
+            src_ref=staged[g].at[pl.ds(dest * slots, slots)],
             dst_ref=landed[g].at[mine],
             send_sem=send_sem.at[g, o],
             recv_sem=recv_sem.at[g, o],
@@ -234,6 +256,9 @@
     for g in range(group_count):
         for o in offsets:
             parcel_copy(g, o).start()
+
+    for copy in keep + loads:
+        copy.wait()
 
     dot_cols = min(256, block_len)
     rows_per = replicas
@@ -260,11 +285,9 @@
 
         steps = [t - 1 for t in times if t > 0]
 
-        source = initial if g == 0 else state
-
         def move(tile, carry):
             cols = pl.ds(pl.multiple_of(tile * piece_len, piece_len), piece_len)
-            y = [source[i, :, cols] for i in range(6)]
+            y = [state[i, :, cols] for i in range(6)]
             drive = noise[:, cols]
             now = coupled[steps[0] * rows_per : (steps[0] + 1) * rows_per, cols]
             for i, s in enumerate(steps):
@@ -280,6 +303,10 @@
 
         lax.fori_loop(0, block_len // piece_len, move, 0)
 
+        if g == group_count - 1:
+            save_state = pltpu.make_async_copy(state, final_hbm, local_sem.at[4])
+            save_state.start()
+
         signal = lax.dot_general(
             potential[: len(steps) * rows_per, :],
             lead[...],
@@ -359,6 +386,7 @@
     sensors_out[...] = gathered[...]
     for o in offsets:
         gather_copy(o).wait_send()
+    save_state.wait()
 
 
 def body(
@@ -384,6 +412,7 @@
     most = max(len(times) for times in TIME_GROUPS) * replicas
     smem = pl.BlockSpec(memory_space=pltpu.SMEM)
     vmem = pl.BlockSpec(memory_space=pltpu.VMEM)
+    anywhere = pl.BlockSpec(memory_space=pl.ANY)
     own_place, *packed = pl.pallas_call(
         functools.partial(pack_kernel, owners, columns, slots),
         out_shape=[jax.ShapeDtypeStruct((tiles,), jnp.int32)]
@@ -393,14 +422,17 @@
             )
             for times in TIME_GROUPS
         ],
-        in_specs=[smem] * 4 + [vmem] * 2,
+        in_specs=[smem] * 4 + [anywhere] * 2,
         out_specs=[smem] + [vmem] * groups,
         scratch_shapes=[
             pltpu.SMEM((owners * slots,), jnp.int32),
             pltpu.SMEM((owners * slots,), jnp.int32),
             pltpu.VMEM((replicas, block_len), jnp.bfloat16),
+            pltpu.VMEM((2, replicas, block_len), jnp.float32),
+            pltpu.VMEM(history.shape, jnp.bfloat16),
+            pltpu.SemaphoreType.DMA((2,)),
         ],
-        compiler_params=pltpu.CompilerParams(vmem_limit_bytes=8 * 1024 * 1024),
+        compiler_params=pltpu.CompilerParams(vmem_limit_bytes=VMEM_BYTES),
         cost_estimate=pl.CostEstimate(flops=0, bytes_accessed=8 * 1024 * 1024, transcendentals=0),
     )(src_group.T, src_sub.T, delays.T, counts, initial, history)
     final, signal = pl.pallas_call(
@@ -409,9 +441,13 @@
             jax.ShapeDtypeStruct(initial.shape, jnp.float32),
             jax.ShapeDtypeStruct((owners, chunk, sensors), jnp.float32),
         ),
-        in_specs=[smem] + [vmem] * (4 + groups),
-        out_specs=(vmem, vmem),
+        in_specs=[smem] + [anywhere] * (4 + groups),
+        out_specs=(anywhere, vmem),
         scratch_shapes=[
+            pltpu.VMEM(initial.shape, jnp.float32),
+            pltpu.VMEM((replicas, block_len), jnp.float32),
+            pltpu.VMEM((tiles * piece_len, block_len), jnp.bfloat16),
+            pltpu.VMEM(lead_field.shape, jnp.bfloat16),
             pltpu.VMEM((most, tiles * piece_len), jnp.bfloat16),
             pltpu.VMEM(((STEPS + 1) * replicas, block_len), jnp.float32),
             pltpu.VMEM((most, block_len), jnp.bfloat16),
@@ -419,6 +455,9 @@
             pltpu.VMEM((owners, chunk, sensors), jnp.float32),
             pltpu.VMEM((columns, chunk, sensors), jnp.float32),
             pltpu.VMEM((owners, chunk, sensors), jnp.float32),
+            pltpu.SemaphoreType.DMA((5,)),
+            pltpu.SemaphoreType.DMA((groups,)),
+            pltpu.SemaphoreType.DMA((groups,)),
             pltpu.SemaphoreType.DMA((groups, owners)),
             pltpu.SemaphoreType.DMA((groups, owners)),
             pltpu.SemaphoreType.DMA((owners,)),
@@ -429,11 +468,15 @@
             pltpu.SemaphoreType.DMA((owners,)),
         ]
         + [
+            pltpu.VMEM((owners * slots, len(times), replicas, piece_len), jnp.bfloat16)
+            for times in TIME_GROUPS
+        ]
+        + [
             pltpu.VMEM((owners * slots + 1, len(times), replicas, piece_len), jnp.bfloat16)
             for times in TIME_GROUPS
         ],
         compiler_params=pltpu.CompilerParams(
-            collective_id=0, has_side_effects=True, vmem_limit_bytes=20 * 1024 * 1024
+            collective_id=0, has_side_effects=True, vmem_limit_bytes=VMEM_BYTES
         ),
     )(
         own_place,

time: 72.3 us -> 64.3 us (0.89)
  local copies, waits for them, and re-layouts: 13.4 us -> 3.63 us
  Pallas kernels: 57.8 us -> 59.7 us
    unnamed x22 -> x2, local copies, waits for them, and re-layouts: 13.4 us -> 3.63 us
    pallas_call x1, Pallas kernels: 4.18 us -> 5.22 us  [body(): pl.pallas_call(functools.partial(pack_kernel, owners, columns, slots), ou...]
    pallas_call x1, Pallas kernels: 53.6 us -> 54.5 us  [body(): pl.pallas_call(functools.partial(kernel, owners, columns, slots), out_sha...]
where the time goes in v2:
time: 64.3 us; the launch traced here: 64 us
  Pallas kernels  59.7 us (93%)
  local copies, waits for them, and re-layouts  3.63 us (6%)
  between operations  0.65 us (1%)
    pallas_call x1, Pallas kernels, body(): pl.pallas_call(functools.partial(kernel, owners, columns, slots), out_sha...  54.5 us
    pallas_call x1, Pallas kernels, body(): pl.pallas_call(functools.partial(pack_kernel, owners, columns, slots), ou...  5.22 us
    unnamed x2, local copies, waits for them, and re-layouts  3.63 us

profile of v2, /device:TPU:0, one launch (start us, length us, event | category | flops | bytes accessed | tf_op | source)
XLA Modules:
  0.0 64.0 jit_solution(17143897013708407038)
XLA Ops:
  0.6 5.2 %shard_map.104 = (s32[24]{0:T(128)}, bf16[24,2,32,128]{3,2,1,0:T(8,128)(2,1)}, bf16[24,2,32,128]{3,2,1,0:T(8,128)(2,1)}, bf16[24,2,32,128]{3,2,1,0:T(8,128)(2,1)}, bf16[24,1,32,128]{3,2,1,0:T(8,128)(2,1)}) custom-call(s32[24,32]{1,0:T(8,128)} %bitcast.9, s32[24,32]{1,0:T(8,128)} %bitcast.10, s32[24,32]{1,0:T(8,128)} %bitcast.11, s32[32]{0:T(128)} %counts.1, ...), custom_call_target="tpu_custom_call" | custom-call | bytes 8388608 | tf_op jit(solution)/shard_map/pallas_call | solution.py:416
  5.9 54.5 %shard_map.105 = (f32[6,32,1024]{2,1,0:T(8,128)}, f32[8,24,128]{2,1,0:T(8,128)}) custom-call(s32[24]{0:T(128)} %get-tuple-element.9.own_place, f32[6,32,1024]{2,1,0:T(8,128)} %initial_hbm.3, f32[32,1024]{1,0:T(8,128)} %noise_hbm.1, bf16[3072,1024]{1,0:T(8,128)(2,1)} %bitcast.7, bf16[128,1024]{1,0:T(8,128)(2,1)} %lead_hbm.1, ...), custom_call_target="tpu_custom_call" | custom-call | tf_op jit(solution)/shard_map/pallas_call | solution.py:438
  60.3 2.1 %copy.13 = f32[6,32,1024]{2,1,0:T(8,128)} copy(f32[6,32,1024]{2,1,0:T(8,128)} %get-tuple-element.18) | data formatting | bytes 1572864
  62.4 1.5 %copy.14 = f32[6,128,32]{1,2,0:T(8,128)} copy(f32[6,128,32]{1,2,0:T(8,128)} %bitcast.8) | data formatting | bytes 196608
